TPU v7x, 32 devices: a whole 2x2x4 slice. The times are simulated.
32 devices in a mesh: grp: 4 (over z), mem: 8 (over y, x, core).
Axes of the slice: x: 2, y: 2, z: 4, core: 2. Of those that a mesh axis runs over, the one named last changes fastest.
Arguments:
- embeddings: bfloat16 [32768, 4096], P(('grp', 'mem')), may hold values from -6 to 6
- local_picks: int32 [4, 64], P('grp', 'mem'), may hold values from 0 to 1023
- second_picks: int32 [4, 16], P('grp'), may hold values from 0 to 63
- final_picks: int32 [16], replicated, may hold values from 0 to 63
Outputs:
- gain_table: float32 [64, 64], P('grp', 'mem')
- final_cover: float32 [32768], P(('grp', 'mem'))
Inputs may be any that keep to these rules, and one draw needn't show every extreme that they name: `local_picks`: entry (g, m * 8 + k) names a row among the 1024 points of device m of group g; repeats may occur. `second_picks`: candidate indices of the group, in greedy order; repeats may occur. `final_picks`: index g * 16 + t names group g's second-round pick t; repeats may occur.
All inputs are finite; a program needn't handle non-finite values.
Results may differ from a plain program's by a relative error of at most 0.0003.
Values may be sent and summed in bfloat16 or wider, within the bound.
A program may use at most 64 MiB of HBM per device.

v0:
```python
import jax
import jax.numpy as jnp
from jax import lax
from jax.sharding import PartitionSpec as P

D = 4096


def per_device(embeddings, local_picks, second_picks, final_picks):
    scaling = float(D) ** (-0.5)
    point_count = embeddings.shape[0]
    local_count = local_picks.shape[1]
    second_list = second_picks[0]
    member = lax.axis_index("mem")
    choose = (local_picks[0][:, None] == lax.iota(jnp.int32, point_count)[None, :]).astype(
        jnp.bfloat16
    )
    own_rows = jnp.dot(choose, embeddings, preferred_element_type=jnp.float32).astype(jnp.bfloat16)

    def similar(other_rows):
        dims = (((1,), (1,)), ((), ()))
        return (
            lax.dot_general(embeddings, other_rows, dims, preferred_element_type=jnp.float32)
            * scaling
        )

    candidates = lax.all_gather(own_rows, "mem", axis=0, tiled=True)
    similar_map = similar(candidates)
    cand_total = candidates.shape[0]
    pick_table = (second_list[:, None] == lax.iota(jnp.int32, cand_total)[None, :]).astype(
        jnp.bfloat16
    )
    winners = jnp.dot(pick_table, candidates, preferred_element_type=jnp.float32).astype(
        jnp.bfloat16
    )
    union_rows = lax.all_gather(winners, "grp", axis=0, tiled=True)
    final_table = (
        final_picks[:, None] == lax.iota(jnp.int32, union_rows.shape[0])[None, :]
    ).astype(jnp.bfloat16)
    final_rows = jnp.dot(final_table, union_rows, preferred_element_type=jnp.float32).astype(
        jnp.bfloat16
    )
    own_block = lax.dynamic_slice_in_dim(similar_map, member * local_count, local_count, 1)
    coverage = jnp.max(own_block, axis=1)
    chosen_cols = jnp.take(similar_map, second_list, axis=1)

    def greedy_step(cover_now, column):
        partial_value = jnp.sum(jnp.maximum(similar_map - cover_now[:, None], 0.0), axis=0)
        return (jnp.maximum(cover_now, column), partial_value)

    _, partials = lax.scan(greedy_step, coverage, chosen_cols.T)
    gain_table = lax.psum_scatter(partials, "mem", scatter_dimension=1, tiled=True) / point_count
    final_cover = jnp.max(similar(final_rows), axis=1)
    return (gain_table, final_cover)


def solution(mesh):
    placed = (P(("grp", "mem"), None), P("grp", "mem"), P("grp", None), P())
    return jax.shard_map(
        per_device,
        mesh=mesh,
        in_specs=placed,
        out_specs=(P("grp", "mem"), P(("grp", "mem"))),
        check_vma=False,
    )
```

profile of v0, /device:TPU:0, one launch (start us, length us, event | category | flops | bytes accessed | tf_op | source)
XLA Modules:
  0.0 75.5 jit_solution(6943562138550951512)
XLA Ops:
  0.6 1.2 %dynamic-slice.4 = u32[1]{0:T(128)} dynamic-slice(u32[32]{0:T(128)} %constant.50, u32[]{:T(128)S(6)} %add.27), dynamic_slice_sizes={1} | dynamic-slice | bytes 12
  2.5 0.7 compare_and_fusion
  3.2 0.7 fusion.7
  3.9 4.8 %convolution_convert_fusion.2 = bf16[8,4096]{1,0:T(8,128)(2,1)S(1)} fusion(bf16[1024,4096]{1,0:T(8,128)(2,1)} %param.6, s32[8]{0:T(128)} %bitcast.25), kind=kOutput, calls=%fused_computation.5 | convolution fusion | flops 67149824 | bytes 8454176 | tf_op jit(solution)/shard_map/dot_general | solution.py:18
  8.7 11.3 %all_gather.6 = bf16[64,4096]{1,0:T(8,128)(2,1)S(1)} all-gather(bf16[8,4096]{1,0:T(8,128)(2,1)S(1)} %convolution_convert_fusion.2), channel_id=1, replica_groups=mesh['grp'=4,'mem'=8] {'mem'}, dimensions={0}, use_global_device_ids=true | all-gather | bytes 589824 | tf_op jit(solution)/shard_map/all_gather | solution.py:27
  20.0 0.2 convolution_convert_fusion.1
  20.3 2.7 %convolution_multiply_fusion = f32[64,1024]{1,0:T(8,128)S(1)} fusion(bf16[64,4096]{1,0:T(8,128)(2,1)S(1)} %all_gather.6, bf16[1024,4096]{1,0:T(8,128)(2,1)S(1)} %copy-done), kind=kOutput, calls=%fused_computation.6 | convolution fusion | flops 536936448 | bytes 9175040 | tf_op jit(solution)/shard_map/dot_general | solution.py:23
  23.0 0.6 gather_fusion
  23.8 4.8 %while.12 = (s32[]{:T(128)}, f32[1024]{0:T(1024)S(1)}, f32[16,64]{1,0:T(8,128)S(1)}, f32[16,1024]{1,0:T(8,128)S(1)}, f32[1024,64]{1,0:T(8,128)S(1)}, /*index=5*/s32[]{:T(128)}, s32[]{:T(128)}) while((s32[]{:T(128)}, f32[1024]{0:T(1024)S(1)}, f32[16,64]{1,0:T(8,128)S(1)}, f32[16,1024]{1,0:T(8,128)S(1)}, f32[1024,64]{1,0:T(8,128)S(1)}, ...), condition=%wide.region_3.4_spmd, body=%wide.region_1.0_spmd.sunk | while | flops 197570 | bytes 287581 | solution.py:51
  23.8 0.2 maximum_reduce_fusion.2
  24.1 0.2 maximum_reduce_fusion.2
  24.4 0.2 maximum_reduce_fusion.2
  24.7 0.2 maximum_reduce_fusion.2
  25.0 0.2 maximum_reduce_fusion.2
  25.3 0.2 maximum_reduce_fusion.2
  25.6 0.2 maximum_reduce_fusion.2
  27.5 0.2 maximum_reduce_fusion.2
  27.8 0.2 maximum_reduce_fusion.2
  28.1 0.2 maximum_reduce_fusion.2
  28.4 0.2 maximum_reduce_fusion.2
  28.7 23.6 %all-reduce = f32[16,64]{0,1:T(8,128)S(1)} all-reduce(f32[16,64]{0,1:T(8,128)S(1)} %copy.9), channel_id=2, replica_groups=mesh['grp'=4,'mem'=8] {'mem'}, use_global_device_ids=true, to_apply=%region_4.5.clone | all-reduce | flops 1024 | bytes 8192
  52.3 0.6 dynamic-slice_multiply_fusion
  52.9 16.2 %all_gather.7 = bf16[64,4096]{1,0:T(8,128)(2,1)S(1)} all-gather(bf16[16,4096]{1,0:T(8,128)(2,1)S(1)} %convolution_convert_fusion.1), channel_id=1, replica_groups=mesh['grp'=4,'mem'=8] {'grp'}, dimensions={0}, use_global_device_ids=true | all-gather | bytes 655360 | tf_op jit(solution)/shard_map/all_gather | solution.py:36
  69.1 6.4 %fusion.2 = f32[1024]{0:T(1024)} fusion(bf16[1024,4096]{1,0:T(8,128)(2,1)} %param.6, bf16[64,4096]{1,0:T(8,128)(2,1)S(1)} %all_gather.7, s32[16]{0:T(128)S(1)} %copy-done.1), kind=kOutput, calls=%fused_computation.9 | convolution fusion | flops 142704640 | bytes 8917056 | tf_op jit(solution)/shard_map/dot_general | solution.py:23
  (65 shorter events, 2.3 us)
Async XLA Ops:
  0.6 19.4 %copy-start.2 = (s32[1,16]{1,0:T(1,128)S(1)}, s32[1,16]{1,0:T(1,128)}, u32[]{:S(2)}) copy-start(s32[1,16]{1,0:T(1,128)} %param.8) | copy-start | bytes 196
  3.9 16.4 %copy-start = (bf16[1024,4096]{1,0:T(8,128)(2,1)S(1)}, bf16[1024,4096]{1,0:T(8,128)(2,1)}, u32[]{:S(2)}) copy-start(bf16[1024,4096]{1,0:T(8,128)(2,1)} %param.6) | copy-start | bytes 25165828
  20.3 48.9 %copy-start.1 = (s32[16]{0:T(128)S(1)}, s32[16]{0:T(128)}, u32[]{:S(2)}) copy-start(s32[16]{0:T(128)} %param.9) | copy-start | bytes 196
where the time goes:
time: 75.8 us; the launch traced here: 75.5 us
  blocking collectives  51.1 us (67%)
  matrix products  14.1 us (19%)
  other arithmetic  5.58 us (7%)
  local copies, waits for them, and re-layouts  2.9 us (4%)
  between operations  1.36 us (2%)
    unnamed x1, blocking collectives  23.6 us
    all_gather x1, blocking collectives, per_device(): union_rows = lax.all_gather(winners, 'grp', axis=0, tiled=True)  16.2 us
    all_gather x1, blocking collectives, per_device(): candidates = lax.all_gather(own_rows, 'mem', axis=0, tiled=True)  11.3 us
    dot_general x2, matrix products, similar(): lax.dot_general(embeddings, other_rows, dims, preferred_element_type=jnp....  9.06 us
    dot_general x1, matrix products, per_device(): jnp.dot(choose, embeddings, preferred_element_type=jnp.float32)  4.78 us
    reduce_sum x16, other arithmetic, greedy_step(): jnp.sum(jnp.maximum(similar_map - cover_now[:, None], 0.0), axis=0)  3.49 us

commit v1 on v0

--- a/solution.py
+++ b/solution.py
@@ -4,6 +4,28 @@
 from jax.sharding import PartitionSpec as P
 
 D = 4096
+
+
+def laid_out(blocks, dim):
+    blocks = jnp.moveaxis(blocks, 0, dim)
+    lengths = blocks.shape
+    return blocks.reshape(*lengths[:dim], lengths[dim] * lengths[dim + 1], *lengths[dim + 2 :])
+
+
+def doubled(value, axis):
+    size = lax.axis_size(axis)
+    blocks = value[None]
+    for level in range(size.bit_length() - 1):
+        apart = 1 << level
+        other = lax.ppermute(blocks, axis, [(i, i ^ apart) for i in range(size)])
+        both = jnp.stack([blocks, other])
+        upper = lax.axis_index(axis) >> level & 1
+        blocks = jnp.where(upper == 0, both, both[::-1]).reshape(-1, *value.shape)
+    return blocks
+
+
+def collect(shard, axis, dim):
+    return laid_out(doubled(shard, axis), dim)
 
 
 def per_device(embeddings, local_picks, second_picks, final_picks):
@@ -33,7 +55,7 @@
     winners = jnp.dot(pick_table, candidates, preferred_element_type=jnp.float32).astype(
         jnp.bfloat16
     )
-    union_rows = lax.all_gather(winners, "grp", axis=0, tiled=True)
+    union_rows = collect(winners, "grp", 0)
     final_table = (
         final_picks[:, None] == lax.iota(jnp.int32, union_rows.shape[0])[None, :]
     ).astype(jnp.bfloat16)

time: 75.8 us -> 62 us (0.82)
  blocking collectives: 51.1 us -> 34.3 us
  starting transfers between devices: 0 us -> 4.3 us
  other arithmetic: 5.58 us -> 4.49 us
    all_gather x1 -> x0, blocking collectives: 16.2 us -> none  [per_device(): union_rows = lax.all_gather(winners, 'grp', axis=0, tiled=True)]
    ppermute x0 -> x2, starting transfers between devices: none -> 4.3 us  [doubled(): other = lax.ppermute(blocks, axis, [(i, i ^ apart) for i in range(size)])]
    unnamed x1, blocking collectives: 23.6 us -> 22.8 us
  transfers between devices with their start and end apart: 0 -> 2, of which waited for: 0 -> 1; matrix products, arithmetic and copies ran while one was open for 0% -> 15% of each run, Pallas kernels for 0% -> 0%
where the time goes in v1:
time: 62 us; the launch traced here: 61.8 us
  blocking collectives  34.3 us (55%)
  matrix products  14.1 us (23%)
  other arithmetic  4.49 us (7%)
  starting transfers between devices  4.3 us (7%)
  local copies, waits for them, and re-layouts  2.23 us (4%)
  between operations  1.44 us (2%)
    unnamed x1, blocking collectives  22.8 us
    all_gather x1, blocking collectives, per_device(): candidates = lax.all_gather(own_rows, 'mem', axis=0, tiled=True)  11.5 us
    dot_general x2, matrix products, similar(): lax.dot_general(embeddings, other_rows, dims, preferred_element_type=jnp....  9.06 us
    dot_general x1, matrix products, per_device(): jnp.dot(choose, embeddings, preferred_element_type=jnp.float32)  4.78 us
    ppermute x2, starting transfers between devices, doubled(): other = lax.ppermute(blocks, axis, [(i, i ^ apart) for i in range(size)])  4.3 us
    reduce_sum x16, other arithmetic, greedy_step(): jnp.sum(jnp.maximum(similar_map - cover_now[:, None], 0.0), axis=0)  3.48 us
  transfers between devices with their start and end apart: 2, of which 1 were waited for; matrix products, arithmetic and copies ran while one was open for 15% of the time, Pallas kernels for 0%

profile of v1, /device:TPU:0, one launch (start us, length us, event | category | flops | bytes accessed | tf_op | source)
XLA Modules:
  0.0 61.8 jit_solution(470589077535064936)
XLA Ops:
  0.7 4.8 %convolution_convert_fusion.2 = bf16[8,4096]{1,0:T(8,128)(2,1)S(1)} fusion(bf16[1024,4096]{1,0:T(8,128)(2,1)} %param.6, s32[8]{0:T(128)} %bitcast.41), kind=kOutput, calls=%fused_computation.5 | convolution fusion | flops 67149824 | bytes 8454176 | tf_op jit(solution)/shard_map/dot_general | solution.py:40
  5.4 11.5 %all_gather.3 = bf16[64,4096]{1,0:T(8,128)(2,1)S(1)} all-gather(bf16[8,4096]{1,0:T(8,128)(2,1)S(1)} %convolution_convert_fusion.2), channel_id=1, replica_groups=mesh['grp'=4,'mem'=8] {'mem'}, dimensions={0}, use_global_device_ids=true | all-gather | bytes 589824 | tf_op jit(solution)/shard_map/all_gather | solution.py:49
  16.9 0.2 convolution_convert_fusion.1
  17.1 1.6 %collective-permute-start = (bf16[1,16,4096]{2,1,0:T(8,128)(2,1)S(1)}, bf16[1,16,4096]{2,1,0:T(8,128)(2,1)S(1)}, u32[]{:S(2)}, u32[]{:S(2)}) collective-permute-start(bf16[1,16,4096]{2,1,0:T(8,128)(2,1)S(1)} %bitcast.35), channel_id=1, source_target_pairs={{0,8},{8,0},{16,24},{24,16},{1,9},{9,1},{17,25},{25,17},{2,10},{10... | collective-permute-start | bytes 393224 | tf_op jit(solution)/shard_map/ppermute | solution.py:20
  18.8 2.7 %convolution_multiply_fusion = f32[64,1024]{1,0:T(8,128)S(1)} fusion(bf16[64,4096]{1,0:T(8,128)(2,1)S(1)} %all_gather.3, bf16[1024,4096]{1,0:T(8,128)(2,1)S(1)} %bitcast.31), kind=kOutput, calls=%fused_computation.6 | convolution fusion | flops 536936448 | bytes 9175040 | tf_op jit(solution)/shard_map/dot_general | solution.py:45
  21.8 0.6 gather_fusion
  22.4 0.5 collective-permute-done
  23.1 2.7 %collective-permute-start.1 = (bf16[2,16,4096]{2,1,0:T(8,128)(2,1)S(1)}, bf16[2,16,4096]{2,1,0:T(8,128)(2,1)S(1)}, u32[]{:S(2)}, u32[]{:S(2)}) collective-permute-start(bf16[2,16,4096]{2,1,0:T(8,128)(2,1)S(1)} %get-tuple-element.51), channel_id=1, source_target_pairs={{0,16},{8,24},{16,0},{24,8},{1,17},{9,25},{17,1},{25,9},{2,18},{10... | collective-permute-start | bytes 786440 | tf_op jit(solution)/shard_map/ppermute | solution.py:20
  25.7 4.8 %while.12 = (s32[]{:T(128)}, f32[1024]{0:T(1024)S(1)}, f32[16,64]{1,0:T(8,128)S(1)}, f32[16,1024]{1,0:T(8,128)S(1)}, f32[1024,64]{1,0:T(8,128)S(1)}, /*index=5*/s32[]{:T(128)}, s32[]{:T(128)}) while((s32[]{:T(128)}, f32[1024]{0:T(1024)S(1)}, f32[16,64]{1,0:T(8,128)S(1)}, f32[16,1024]{1,0:T(8,128)S(1)}, f32[1024,64]{1,0:T(8,128)S(1)}, ...), condition=%wide.region_3.4_spmd, body=%wide.region_1.3_spmd.sunk | while | flops 197570 | bytes 287573 | solution.py:73
  26.0 0.2 maximum_reduce_fusion.2
  26.3 0.2 maximum_reduce_fusion.2
  26.6 0.2 maximum_reduce_fusion.2
  26.9 0.2 maximum_reduce_fusion.2
  27.2 0.2 maximum_reduce_fusion.2
  27.5 0.2 maximum_reduce_fusion.2
  27.8 0.2 maximum_reduce_fusion.2
  29.3 0.2 maximum_reduce_fusion.2
  29.6 0.2 maximum_reduce_fusion.2
  29.9 0.2 maximum_reduce_fusion.2
  30.2 0.2 maximum_reduce_fusion.2
  30.6 0.6 dynamic-slice.4
  31.9 22.8 %all-reduce = f32[16,64]{0,1:T(8,128)S(1)} all-reduce(f32[16,64]{0,1:T(8,128)S(1)} %copy.9), channel_id=2, replica_groups=mesh['grp'=4,'mem'=8] {'mem'}, use_global_device_ids=true, to_apply=%region_4.5.clone | all-reduce | flops 1024 | bytes 8192
  54.7 0.6 dynamic-slice_multiply_fusion
  55.4 6.4 %fusion.2 = f32[1024]{0:T(1024)} fusion(bf16[1024,4096]{1,0:T(8,128)(2,1)} %param.6, bf16[64,4096]{1,0:T(8,128)(2,1)S(1)} %bitcast.34, s32[16]{0:T(128)S(1)} %copy-done), kind=kOutput, calls=%fused_computation.9 | convolution fusion | flops 142704640 | bytes 8917056 | tf_op jit(solution)/shard_map/dot_general | solution.py:45
  (77 shorter events, 2.6 us)
Async XLA Ops:
  0.6 18.2 %slice-start = ((s8[8388608]{0:T(1024)(128)(4,1)}), s8[4194304]{0:T(1024)(128)(4,1)S(1)}, s32[]{:S(2)}) async-start(s8[8388608]{0:T(1024)(128)(4,1)} %bitcast.30), calls=%async_computation | async-start | bytes 8388608
  0.6 16.3 %copy-start.1 = (s32[1,16]{1,0:T(1,128)S(1)}, s32[1,16]{1,0:T(1,128)}, u32[]{:S(2)}) copy-start(s32[1,16]{1,0:T(1,128)} %param.8) | copy-start | bytes 196
  0.7 18.1 %slice-start.1 = ((s8[8388608]{0:T(1024)(128)(4,1)}), s8[4194304]{0:T(1024)(128)(4,1)S(1)}, s32[]{:S(2)}) async-start(s8[8388608]{0:T(1024)(128)(4,1)} %bitcast.30), calls=%async_computation.1 | async-start | bytes 8388608
  17.1 5.8 %collective-permute-start = (bf16[1,16,4096]{2,1,0:T(8,128)(2,1)S(1)}, bf16[1,16,4096]{2,1,0:T(8,128)(2,1)S(1)}, u32[]{:S(2)}, u32[]{:S(2)}) collective-permute-start(bf16[1,16,4096]{2,1,0:T(8,128)(2,1)S(1)} %bitcast.35), channel_id=1, source_target_pairs={{0,8},{8,0},{16,24},{24,16},{1,9},{9,1},{17,25},{25,17},{2,10},{10... | collective-permute-start | bytes 393224 | tf_op jit(solution)/shard_map/ppermute | solution.py:20
  18.8 11.8 %copy-start.2 = (u32[32]{0:T(128)S(1)}, u32[32]{0:T(128)}, u32[]{:S(2)}) copy-start(u32[32]{0:T(128)} %constant.56) | copy-start | bytes 388
  21.5 34.0 %copy-start = (s32[16]{0:T(128)S(1)}, s32[16]{0:T(128)}, u32[]{:S(2)}) copy-start(s32[16]{0:T(128)} %param.9) | copy-start | bytes 196
  23.1 32.2 %collective-permute-start.1 = (bf16[2,16,4096]{2,1,0:T(8,128)(2,1)S(1)}, bf16[2,16,4096]{2,1,0:T(8,128)(2,1)S(1)}, u32[]{:S(2)}, u32[]{:S(2)}) collective-permute-start(bf16[2,16,4096]{2,1,0:T(8,128)(2,1)S(1)} %get-tuple-element.51), channel_id=1, source_target_pairs={{0,16},{8,24},{16,0},{24,8},{1,17},{9,25},{17,1},{25,9},{2,18},{10... | collective-permute-start | bytes 786440 | tf_op jit(solution)/shard_map/ppermute | solution.py:20
